TPU v7x, 256 devices: a whole 4x4x8 slice. The times are simulated.
256 devices in a mesh: section: 4 (over y_lo, core), expert: 64 (over y_hi, x, z).
Axes of the slice: x: 4, y: 4 (y_hi: 2, y_lo: 2; y = y_hi * 2 + y_lo), z: 8, core: 2. Of those that a mesh axis runs over, the one named last changes fastest.
Arguments:
- activations: bfloat16 [4, 2048, 4096], P('section', 'expert'), may hold values from -6 to 6
- norm_gain: float32 [4, 4096], P('section'), may hold values from 0.25 to 1.75
- in_proj: bfloat16 [4, 4096, 40960], P('section', None, 'expert'), may hold values from -0.09375 to 0.09375
- out_proj: bfloat16 [4, 40960, 4096], P('section', 'expert'), may hold values from -0.078125 to 0.078125
- expert_ids: int32 [4, 2048, 1], P('section', 'expert'), may hold values from 0 to 7; in each aligned block of 32 rows (0 to 31, 32 to 63, ..., all dimensions but the last counted through in order) at most 8 rows name the same one
Outputs:
- passed: bfloat16 [4, 2048, 4096], P('section', 'expert')
Inputs may be any that keep to these rules, and one draw needn't show every extreme that they name: `expert_ids`: within the 32 rows of one device (aligned blocks of 32 rows along the token dimension of each layer), no expert is named by more than 8 rows.
All inputs are finite; a program needn't handle non-finite values.
Results may differ from a plain program's by a relative error of at most 0.0047.
Values may be sent and summed in bfloat16 or wider, within the bound.
A program may use at most 64 MiB of HBM per device.

v0:
```python
import functools

import jax
import jax.numpy as jnp
from jax import lax
from jax.experimental import pallas as pl
from jax.experimental.pallas import tpu as pltpu
from jax.sharding import PartitionSpec as P

EXPERTS = 8
SLOTS = 5
MESH = pl.DeviceIdType.MESH
F32, BF16 = jnp.float32, jnp.bfloat16

epsilon = 1e-06


def divisor(size, most):
    return max(k for k in range(128, most + 1, 128) if size % k == 0)


def placement(routed, ranks, capacity, groups, count):
    row = lax.broadcasted_iota(jnp.int32, (count * capacity, routed.shape[1]), 0)
    owner = row // (capacity * groups)
    return jnp.where((owner == routed) & (row % capacity == ranks), 1.0, 0.0).astype(F32)


def kernel(
    sections, n, capacity, act_hbm, gain_hbm, ids_hbm, first_hbm, second_hbm, out,
    act, gain, ids, first, second, normed, packed, received, total, hidden, outgoing, returned,
    where_to, residual, where_from,
    small_sem, first_sem, second_sem, pass_send, pass_recv, send_sem, recv_sem, back_send, back_recv,
):
    section, me = lax.axis_index("section"), lax.axis_index("expert")
    following = lax.rem(section + 1, sections)
    groups = n // EXPERTS
    tokens, width = act.shape
    ff = hidden.shape[1]
    chunks, depth = packed.shape[0], packed.shape[3]
    tiles, columns = outgoing.shape[0], outgoing.shape[3]
    loads = chunks + tiles

    def load(step, is_first):
        if is_first:
            rows = pl.ds(pl.multiple_of(step * depth, depth), depth)
            slot = lax.rem(step, SLOTS)
            return pltpu.make_async_copy(first_hbm.at[0, rows, :], first.at[slot], first_sem.at[slot])
        cols = pl.ds(pl.multiple_of(step * columns, columns), columns)
        slot = lax.rem(step, SLOTS)
        return pltpu.make_async_copy(second_hbm.at[0, :, cols], second.at[slot], second_sem.at[slot])

    smalls = [
        pltpu.make_async_copy(act_hbm.at[0], act, small_sem.at[0]),
        pltpu.make_async_copy(gain_hbm, gain, small_sem.at[1]),
        pltpu.make_async_copy(ids_hbm, ids, small_sem.at[2]),
    ]
    barrier = pltpu.get_barrier_semaphore()
    shifts = (0, sections - 1)
    for shift in shifts:
        peer_section = lax.rem(section + shift, sections)

        def greet(i, carry):
            peer = lax.rem(me + i, n)
            pl.semaphore_signal(barrier, inc=1, device_id=(peer_section, peer), device_id_type=MESH)
            return carry

        lax.fori_loop(1 if shift == 0 else 0, n, greet, 0)

    for copy in smalls:
        copy.start()
    for step in range(SLOTS):
        load(jnp.int32(step), True).start()

    for copy in smalls:
        copy.wait()
    floats = act[...].astype(F32)
    scale = lax.rsqrt(jnp.mean(floats * floats, axis=-1, keepdims=True) + epsilon)
    normed[...] = (floats * scale * gain[...]).astype(BF16)
    routed = ids[...]
    expert = lax.broadcasted_iota(jnp.int32, (EXPERTS, tokens), 0)
    onehot = jnp.where(expert == routed, 1.0, 0.0).astype(F32)
    earlier = lax.broadcasted_iota(jnp.int32, (tokens, tokens), 0) < lax.broadcasted_iota(
        jnp.int32, (tokens, tokens), 1
    )
    before = jnp.dot(
        onehot.astype(BF16), jnp.where(earlier, 1.0, 0.0).astype(BF16), preferred_element_type=F32
    )
    ranks = jnp.sum(before * onehot, axis=0, keepdims=True).astype(jnp.int32)
    placing = placement(routed, ranks, capacity, 1, EXPERTS).astype(BF16)
    back = placement(routed, ranks, capacity, groups, where_to.shape[1] // capacity)
    where_to[...] = back.T.astype(BF16)

    pl.semaphore_wait(barrier, len(shifts) * n - 1)

    half = n // 2
    for c in range(chunks):
        block = jnp.dot(placing, normed[:, c * depth:(c + 1) * depth], preferred_element_type=F32)
        packed[c] = block.astype(BF16).reshape(EXPERTS, capacity, depth)

        def dispatch(i, carry):
            step = (i + 1) // 2
            peer = lax.rem(me + half + jnp.where(lax.rem(i, 2) == 0, step, n - step), n)
            pltpu.make_async_remote_copy(
                src_ref=packed.at[c, peer // groups],
                dst_ref=received.at[c, me],
                send_sem=send_sem.at[c],
                recv_sem=recv_sem.at[c],
                device_id=(section, peer),
                device_id_type=MESH,
            ).start()
            return carry

        lax.fori_loop(0, n - 1, dispatch, 0)
        pltpu.make_async_copy(packed.at[c, me // groups], received.at[c, me], recv_sem.at[c]).start()

    passes = [
        pltpu.make_async_remote_copy(
            src_ref=src, dst_ref=dst, send_sem=pass_send.at[k], recv_sem=pass_recv.at[k],
            device_id=(following, me), device_id_type=MESH,
        )
        for k, (src, dst) in enumerate(((act, residual), (where_to, where_from)))
    ]
    for copy in passes:
        copy.start()

    sub = divisor(ff, 5120)

    def multiply(c, kind):
        load(c, True).wait()
        pltpu.make_async_copy(received.at[c], received.at[c], recv_sem.at[c]).wait()
        slot = lax.rem(c, SLOTS)
        rows = received[c].reshape(n * capacity, depth)

        def part(j, carry):
            cols = pl.ds(pl.multiple_of(j * sub, sub), sub)
            value = jnp.dot(rows, first[slot, :, cols], preferred_element_type=F32)
            if kind != "start":
                value = value + total[:, cols]
            if kind == "end":
                hidden[:, cols] = jax.nn.gelu(value, approximate=True).astype(BF16)
            else:
                total[:, cols] = value
            return carry

        lax.fori_loop(0, ff // sub, part, 0)

    def more(step):
        @pl.when(step < chunks)
        def _():
            load(step, True).start()

        @pl.when((step >= chunks) & (step < loads))
        def _():
            load(step - chunks, False).start()

    multiply(jnp.int32(0), "start")
    more(jnp.int32(SLOTS))

    def middle(c, carry):
        multiply(c, "middle")
        more(c + SLOTS)
        return carry

    lax.fori_loop(1, chunks - 1, middle, 0)
    multiply(jnp.int32(chunks - 1), "end")
    more(jnp.int32(chunks - 1 + SLOTS))

    sub_out = divisor(columns, 512)

    def tile(t, carry):
        load(t, False).wait()
        slot = lax.rem(t, SLOTS)
        for j in range(columns // sub_out):
            cols = slice(j * sub_out, (j + 1) * sub_out)
            piece = jnp.dot(hidden[...], second[slot, :, cols], preferred_element_type=F32)
            outgoing[t, :, :, cols] = piece.astype(BF16).reshape(n, capacity, sub_out)
        more(t + chunks + SLOTS)

        def give(i, inner):
            step = (i + 1) // 2
            peer = lax.rem(me + half + jnp.where(lax.rem(i, 2) == 0, step, n - step), n)
            pltpu.make_async_remote_copy(
                src_ref=outgoing.at[t, peer],
                dst_ref=returned.at[t, me],
                send_sem=back_send.at[t],
                recv_sem=back_recv.at[t],
                device_id=(following, peer),
                device_id_type=MESH,
            ).start()
            return inner

        lax.fori_loop(0, n, give, 0)
        return carry

    lax.fori_loop(0, tiles, tile, 0)

    for copy in passes:
        copy.wait()
    picks = where_from[:, :n * capacity]

    def combine(t, carry):
        pltpu.make_async_copy(returned.at[t], returned.at[t], back_recv.at[t]).wait()
        cols = pl.ds(pl.multiple_of(t * columns, columns), columns)
        mixed = jnp.dot(picks, returned[t].reshape(n * capacity, columns), preferred_element_type=F32)
        out[0, :, cols] = (residual[:, cols].astype(F32) + mixed).astype(BF16)
        return carry

    lax.fori_loop(0, tiles, combine, 0)

    def finish(t, carry):
        pltpu.make_async_copy(outgoing.at[t], outgoing.at[t], back_send.at[t]).wait()
        return carry

    lax.fori_loop(0, tiles, finish, 0)

    def drain(c, carry):
        done = received.at[c, pl.ds(0, n - 1)]
        pltpu.make_async_copy(done, done, send_sem.at[c]).wait()
        return carry

    lax.fori_loop(0, chunks, drain, 0)


def per_device(sections, n, activations, norm_gain, in_proj, out_proj, expert_ids):
    tokens, width = activations.shape[1:]
    ff = in_proj.shape[2]
    capacity = 2 * tokens // EXPERTS
    depth = divisor(width, 512)
    columns = divisor(width, 512)
    chunks, tiles = width // depth, width // columns
    rows = n * capacity
    lanes = max(128, rows)
    dma = pltpu.SemaphoreType.DMA
    return pl.pallas_call(
        functools.partial(kernel, sections, n, capacity),
        out_shape=pltpu.VMEM(activations.shape, activations.dtype),
        in_specs=[pl.BlockSpec(memory_space=pl.ANY)] * 5,
        out_specs=pl.BlockSpec(memory_space=pltpu.VMEM),
        scratch_shapes=[
            pltpu.VMEM((tokens, width), BF16),
            pltpu.VMEM((1, width), F32),
            pltpu.VMEM((1, tokens), jnp.int32),
            pltpu.VMEM((SLOTS, depth, ff), BF16),
            pltpu.VMEM((SLOTS, ff, columns), BF16),
            pltpu.VMEM((tokens, width), BF16),
            pltpu.VMEM((chunks, EXPERTS, capacity, depth), BF16),
            pltpu.VMEM((chunks, n, capacity, depth), BF16),
            pltpu.VMEM((rows, ff), F32),
            pltpu.VMEM((rows, ff), BF16),
            pltpu.VMEM((tiles, n, capacity, columns), BF16),
            pltpu.VMEM((tiles, n, capacity, columns), BF16),
            pltpu.VMEM((tokens, lanes), BF16),
            pltpu.VMEM((tokens, width), BF16),
            pltpu.VMEM((tokens, lanes), BF16),
            dma((3,)),
            dma((SLOTS,)),
            dma((SLOTS,)),
            dma((2,)),
            dma((2,)),
            dma((chunks,)),
            dma((chunks,)),
            dma((tiles,)),
            dma((tiles,)),
        ],
        compiler_params=pltpu.CompilerParams(
            collective_id=0, has_side_effects=True, vmem_limit_bytes=62 * 1024 * 1024
        ),
    )(activations, norm_gain, expert_ids.reshape(1, tokens), in_proj, out_proj)


def solution(mesh):
    return jax.shard_map(
        functools.partial(per_device, mesh.shape["section"], mesh.shape["expert"]),
        mesh=mesh,
        in_specs=(
            P("section", "expert", None),
            P("section", None),
            P("section", None, "expert"),
            P("section", "expert", None),
            P("section", "expert", None),
        ),
        out_specs=P("section", "expert", None),
        check_vma=False,
    )
```

profile of v0, /device:TPU:1, one launch (start us, length us, event | category | flops | bytes accessed | tf_op | source)
XLA Modules:
  0.0 206.0 jit_solution(17830571551591665903)
XLA Ops:
  0.0 205.3 %shard_map.55 = bf16[1,32,4096]{2,1,0:T(8,128)(2,1)S(1)} custom-call(bf16[1,32,4096]{2,1,0:T(8,128)(2,1)} %act_hbm.1, f32[1,4096]{1,0:T(1,128)} %gain_hbm.1, s32[1,32]{1,0:T(1,128)} %bitcast.1, bf16[1,4096,640]{2,1,0:T(8,128)(2,1)} %first_hbm.1, bf16[1,640,4096]{2,1,0:T(8,128)(2,1)} %second_hbm.1), custom_call_target="tpu_custom_call" | custom-call | tf_op jit(solution)/shard_map/pallas_call | solution.py:234
  205.3 0.7 copy.7
where the time goes:
time: 206 us
  Pallas kernels  205 us (100%)
    pallas_call x1, Pallas kernels, per_device(): pl.pallas_call(functools.partial(kernel, sections, n, capacity), out_shap...  205 us

commit v1 on v0

v1 whole, which is shorter than its diff:
```python
import functools

import jax
import jax.numpy as jnp
from jax import lax
from jax.experimental import pallas as pl
from jax.experimental.pallas import tpu as pltpu
from jax.sharding import PartitionSpec as P

EXPERTS = 8
RING = 8
NX = 4
NEAR = ((0, 0), (0, 1), (0, 3), (1, 0), (0, 2), (1, 1), (1, 3), (1, 2))
MESH = pl.DeviceIdType.MESH
F32, BF16 = jnp.float32, jnp.bfloat16

epsilon = 1e-06


def neighbour(group, o):
    dy, dx = NEAR[o]
    return lax.rem(group // NX + dy, EXPERTS // NX) * NX + lax.rem(group % NX + dx, NX)


def mirrored(o):
    dy, dx = NEAR[o]
    return NEAR.index((dy, (NX - dx) % NX))


def placement(routed, ranks, capacity, group, rows):
    row = lax.broadcasted_iota(jnp.int32, (rows, routed.shape[1]), 0)
    place = row // capacity
    owner = jnp.full_like(place, -1)
    for o in range(EXPERTS):
        owner = jnp.where(place == o, neighbour(group, o), owner)
    return jnp.where((owner == routed) & (row % capacity == ranks), 1.0, 0.0).astype(F32)


def arrived(ref, sem):
    pltpu.make_async_copy(ref, ref, sem).wait()


def kernel(
    sections, n, capacity, act_hbm, gain_hbm, ids_hbm, first_hbm, second_hbm, out,
    act, gain, ids, first, second, normed, packed, gathered, hidden, partial, sending, arriving, summed, returned,
    where_to, residual, where_from,
    small_sem, weight_sem, pass_send, pass_recv, give_send, ring_send, ring_recv, sum_recv, back_send, back_recv,
):
    section, me = lax.axis_index("section"), lax.axis_index("expert")
    following, leading = lax.rem(section + 1, sections), lax.rem(section + sections - 1, sections)
    group, z = me // RING, lax.rem(me, RING)
    tokens, width = act.shape
    ff = hidden.shape[1]
    rows = EXPERTS * capacity

    def along(k):
        return lax.rem(z + k, RING)

    def on_ring(k):
        return (section, group * RING + along(k))

    def in_plane(o, which):
        return (which, neighbour(group, o) * RING + z)

    smalls = [
        pltpu.make_async_copy(act_hbm.at[0], act, small_sem.at[0]),
        pltpu.make_async_copy(gain_hbm, gain, small_sem.at[1]),
        pltpu.make_async_copy(ids_hbm, ids, small_sem.at[2]),
    ]
    weights = [
        pltpu.make_async_copy(first_hbm.at[0], first, weight_sem.at[0]),
        pltpu.make_async_copy(second_hbm.at[0], second, weight_sem.at[1]),
    ]
    for copy in smalls:
        copy.start()
    barrier = pltpu.get_barrier_semaphore()
    greeted = [in_plane(o, section) for o in range(1, EXPERTS)] + [on_ring(1), on_ring(RING - 1)]
    greeted += [in_plane(o, leading) for o in range(EXPERTS)]
    for peer in greeted:
        pl.semaphore_signal(barrier, inc=1, device_id=peer, device_id_type=MESH)
    for copy in smalls:
        copy.wait()
    for copy in weights:
        copy.start()

    floats = act[...].astype(F32)
    scale = lax.rsqrt(jnp.mean(floats * floats, axis=-1, keepdims=True) + epsilon)
    normed[...] = (floats * scale * gain[...]).astype(BF16)
    routed = ids[...]
    expert = lax.broadcasted_iota(jnp.int32, (EXPERTS, tokens), 0)
    onehot = jnp.where(expert == routed, 1.0, 0.0).astype(F32)
    earlier = lax.broadcasted_iota(jnp.int32, (tokens, tokens), 0) < lax.broadcasted_iota(
        jnp.int32, (tokens, tokens), 1
    )
    before = jnp.dot(
        onehot.astype(BF16), jnp.where(earlier, 1.0, 0.0).astype(BF16), preferred_element_type=F32
    )
    ranks = jnp.sum(before * onehot, axis=0, keepdims=True).astype(jnp.int32)
    placing = placement(routed, ranks, capacity, group, where_to.shape[1])
    where_to[...] = placing.T.astype(BF16)
    placing = placing[:rows].astype(BF16)
    step = 512
    for c in range(width // step):
        cols = slice(c * step, (c + 1) * step)
        block = jnp.dot(placing, normed[:, cols], preferred_element_type=F32)
        packed[:, :, cols] = block.astype(BF16).reshape(EXPERTS, capacity, step)
    gathered[z, 0] = packed[0]

    pl.semaphore_wait(barrier, len(greeted))

    def forward(block, o, k, way):
        pltpu.make_async_remote_copy(
            src_ref=gathered.at[block, o], dst_ref=gathered.at[block, o],
            send_sem=ring_send.at[way], recv_sem=ring_recv.at[block, o],
            device_id=on_ring(k), device_id_type=MESH,
        ).start()

    forward(z, 0, 1, 0)
    forward(z, 0, RING - 1, 1)
    for o in range(1, EXPERTS):
        pltpu.make_async_remote_copy(
            src_ref=packed.at[o], dst_ref=gathered.at[z, mirrored(o)],
            send_sem=give_send.at[0], recv_sem=ring_recv.at[z, mirrored(o)],
            device_id=in_plane(o, section), device_id_type=MESH,
        ).start()
    passes = [
        pltpu.make_async_remote_copy(
            src_ref=src, dst_ref=dst, send_sem=pass_send.at[k], recv_sem=pass_recv.at[k],
            device_id=(following, me), device_id_type=MESH,
        )
        for k, (src, dst) in enumerate(((act, residual), (where_to, where_from)))
    ]
    for copy in passes:
        copy.start()

    def spread(o, carry):
        arrived(gathered.at[z, o], ring_recv.at[z, o])
        forward(z, o, 1, 0)
        forward(z, o, RING - 1, 1)
        return carry

    lax.fori_loop(1, EXPERTS, spread, 0)
    for copy in weights:
        copy.wait()

    def pass_on(way, j, o, add):
        distance = RING // 2 - j
        block = along(distance if way == 0 else RING - distance)
        value = partial[block, o]
        if add:
            arrived(arriving.at[way, j - 1, o], sum_recv.at[way, j - 1, o])
            value = value + arriving[way, j - 1, o].astype(F32)
        sending[way, j, o] = value.astype(BF16)
        pltpu.make_async_remote_copy(
            src_ref=sending.at[way, j, o], dst_ref=arriving.at[way, j, o],
            send_sem=ring_send.at[way], recv_sem=sum_recv.at[way, j, o],
            device_id=on_ring(1 if way == 0 else RING - 1), device_id_type=MESH,
        ).start()

    half = RING // 2

    def gather(k, carry):
        left, right = along(RING - k), along(k)

        def hop(o, inner):
            arrived(gathered.at[left, o], ring_recv.at[left, o])

            @pl.when((k < half - 1) | ((k == half - 1) & (o % 2 == 0)))
            def _():
                forward(left, o, 1, 0)

            @pl.when(k < half)
            def _():
                arrived(gathered.at[right, o], ring_recv.at[right, o])

            @pl.when((k < half - 1) | ((k == half - 1) & (o % 2 == 1)))
            def _():
                forward(right, o, RING - 1, 1)

            return inner

        lax.fori_loop(0, EXPERTS, hop, 0)
        other = jnp.where(k < half, right, z)
        inputs = jnp.concatenate(
            [gathered[left].reshape(rows, width), gathered[other].reshape(rows, width)], axis=0
        )
        value = jnp.dot(inputs, first[...], preferred_element_type=F32)
        hidden[...] = jax.nn.gelu(value, approximate=True).astype(BF16)

        def tile(t, inner):
            cols = pl.ds(pl.multiple_of(t * step, step), step)
            piece = jnp.dot(hidden[...], second[:, cols], preferred_element_type=F32)
            piece = piece.reshape(2, EXPERTS, capacity, step)
            partial[left, :, :, cols] = piece[0]
            partial[other, :, :, cols] = piece[1]
            return inner

        lax.fori_loop(0, width // step, tile, 0)

        @pl.when(k == half - 1)
        def _():
            def early(i, inner):
                pass_on(0, 1, EXPERTS - 1 - 2 * i, False)
                pass_on(1, 1, EXPERTS - 2 - 2 * i, False)
                return inner

            lax.fori_loop(0, EXPERTS // 2, early, 0)

        return carry

    lax.fori_loop(1, half + 1, gather, 0)

    def start(i, carry):
        pass_on(0, 0, EXPERTS - 2 - 2 * i, False)
        pass_on(1, 0, EXPERTS - 1 - 2 * i, False)
        return carry

    lax.fori_loop(0, EXPERTS // 2, start, 0)

    def second_hop(i, carry):
        pass_on(0, 1, EXPERTS - 2 - 2 * i, True)
        pass_on(1, 1, EXPERTS - 1 - 2 * i, True)
        return carry

    lax.fori_loop(0, EXPERTS // 2, second_hop, 0)
    for j in range(2, half):
        def later(i, carry):
            pass_on(0, j, EXPERTS - 1 - i, True)
            pass_on(1, j, EXPERTS - 1 - i, True)
            return carry

        lax.fori_loop(0, EXPERTS, later, 0)

    for o in reversed(range(EXPERTS)):
        value = partial[z, o]
        for way in range(2):
            arrived(arriving.at[way, half - 1, o], sum_recv.at[way, half - 1, o])
            value = value + arriving[way, half - 1, o].astype(F32)
        summed[o] = value.astype(BF16)
        pltpu.make_async_remote_copy(
            src_ref=summed.at[o], dst_ref=returned.at[mirrored(o)],
            send_sem=back_send.at[0], recv_sem=back_recv.at[mirrored(o)],
            device_id=in_plane(o, following), device_id_type=MESH,
        ).start()

    for copy in passes:
        copy.wait()
    for o in reversed(range(EXPERTS)):
        arrived(returned.at[o], back_recv.at[o])
    picks = where_from[:, :rows]
    for c in range(width // step):
        cols = slice(c * step, (c + 1) * step)
        mixed = jnp.dot(picks, returned[:, :, cols].reshape(rows, step), preferred_element_type=F32)
        out[0, :, cols] = (residual[:, cols].astype(F32) + mixed).astype(BF16)

    arrived(packed.at[pl.ds(1, EXPERTS - 1)], give_send.at[0])
    for way in range(2):
        arrived(gathered.at[pl.ds(0, RING - 1)], ring_send.at[way])
    arrived(summed, back_send.at[0])


def per_device(sections, n, activations, norm_gain, in_proj, out_proj, expert_ids):
    tokens, width = activations.shape[1:]
    ff = in_proj.shape[2]
    capacity = 2 * tokens // EXPERTS
    rows = EXPERTS * capacity
    dma = pltpu.SemaphoreType.DMA
    half = RING // 2
    return pl.pallas_call(
        functools.partial(kernel, sections, n, capacity),
        out_shape=pltpu.VMEM(activations.shape, activations.dtype),
        in_specs=[pl.BlockSpec(memory_space=pl.ANY)] * 5,
        out_specs=pl.BlockSpec(memory_space=pltpu.VMEM),
        scratch_shapes=[
            pltpu.VMEM((tokens, width), BF16),
            pltpu.VMEM((1, width), F32),
            pltpu.VMEM((1, tokens), jnp.int32),
            pltpu.VMEM((width, ff), BF16),
            pltpu.VMEM((ff, width), BF16),
            pltpu.VMEM((tokens, width), BF16),
            pltpu.VMEM((EXPERTS, capacity, width), BF16),
            pltpu.VMEM((RING, EXPERTS, capacity, width), BF16),
            pltpu.VMEM((2 * rows, ff), BF16),
            pltpu.VMEM((RING, EXPERTS, capacity, width), F32),
            pltpu.VMEM((2, half, EXPERTS, capacity, width), BF16),
            pltpu.VMEM((2, half, EXPERTS, capacity, width), BF16),
            pltpu.VMEM((EXPERTS, capacity, width), BF16),
            pltpu.VMEM((EXPERTS, capacity, width), BF16),
            pltpu.VMEM((tokens, 128), BF16),
            pltpu.VMEM((tokens, width), BF16),
            pltpu.VMEM((tokens, 128), BF16),
            dma((3,)),
            dma((2,)),
            dma((2,)),
            dma((2,)),
            dma((1,)),
            dma((2,)),
            dma((RING, EXPERTS)),
            dma((2, half, EXPERTS)),
            dma((1,)),
            dma((EXPERTS,)),
        ],
        compiler_params=pltpu.CompilerParams(
            collective_id=0, has_side_effects=True, vmem_limit_bytes=62 * 1024 * 1024
        ),
    )(activations, norm_gain, expert_ids.reshape(1, tokens), in_proj, out_proj)


def solution(mesh):
    return jax.shard_map(
        functools.partial(per_device, mesh.shape["section"], mesh.shape["expert"]),
        mesh=mesh,
        in_specs=(
            P("section", "expert", None),
            P("section", None),
            P("section", None, "expert"),
            P("section", "expert", None),
            P("section", "expert", None),
        ),
        out_specs=P("section", "expert", None),
        check_vma=False,
    )
```

time: 206 us -> 99.8 us (0.48)
  Pallas kernels: 205 us -> 99 us
    pallas_call x1, Pallas kernels: 205 us -> 99 us  [per_device(): pl.pallas_call(functools.partial(kernel, sections, n, capacity), out_shap...]
where the time goes in v1:
time: 99.8 us; the launch traced here: 99.7 us
  Pallas kernels  99 us (99%)
    pallas_call x1, Pallas kernels, per_device(): pl.pallas_call(functools.partial(kernel, sections, n, capacity), out_shap...  99 us

profile of v1, /device:TPU:1, one launch (start us, length us, event | category | flops | bytes accessed | tf_op | source)
XLA Modules:
  0.0 99.7 jit_solution(18162970675040180578)
XLA Ops:
  0.0 99.0 %shard_map.55 = bf16[1,32,4096]{2,1,0:T(8,128)(2,1)S(1)} custom-call(bf16[1,32,4096]{2,1,0:T(8,128)(2,1)} %act_hbm.1, f32[1,4096]{1,0:T(1,128)} %gain_hbm.1, s32[1,32]{1,0:T(1,128)} %bitcast.1, bf16[1,4096,640]{2,1,0:T(8,128)(2,1)} %first_hbm.1, bf16[1,640,4096]{2,1,0:T(8,128)(2,1)} %second_hbm.1), custom_call_target="tpu_custom_call" | custom-call | tf_op jit(solution)/shard_map/pallas_call | solution.py:269
  99.0 0.7 copy.7

commit v2 on v1

v2 whole, which is shorter than its diff:
```python
import functools

import jax
import jax.numpy as jnp
from jax import lax
from jax.experimental import pallas as pl
from jax.experimental.pallas import tpu as pltpu
from jax.sharding import PartitionSpec as P

EXPERTS = 8
RING = 8
NX = 4
FLAT = 2048
PIECES = 4
LANES = 128
STEP = 512
NEAR = ((0, 0), (0, 1), (0, 3), (1, 0), (0, 2), (1, 1), (1, 3), (1, 2))
MESH = pl.DeviceIdType.MESH
F32, BF16 = jnp.float32, jnp.bfloat16

epsilon = 1e-06


def neighbour(group, o):
    dy, dx = NEAR[o]
    return lax.rem(group // NX + dy, EXPERTS // NX) * NX + lax.rem(group % NX + dx, NX)


def mirrored(o):
    dy, dx = NEAR[o]
    return NEAR.index((dy, (NX - dx) % NX))


def placement(routed, ranks, capacity, group, rows):
    row = lax.broadcasted_iota(jnp.int32, (rows, routed.shape[1]), 0)
    place = row // capacity
    owner = jnp.full_like(place, -1)
    for o in range(EXPERTS):
        owner = jnp.where(place == o, neighbour(group, o), owner)
    return jnp.where((owner == routed) & (row % capacity == ranks), 1.0, 0.0).astype(F32)


def arrived(ref, sem):
    pltpu.make_async_copy(ref, ref, sem).wait()


def kernel(
    sections, n, capacity, act_hbm, gain_hbm, ids_hbm, first_hbm, second_hbm, out,
    act, gain, ids, first, second, normed, packed, slots, flat, spread_out, spread_in, hidden,
    partial, sending, arriving, summed, returned,
    parts_out, parts_in, whole, flat_sending, flat_arriving, flat_summed, flat_returned,
    where_to, residual, where_from,
    small_sem, weight_sem, pass_send, pass_recv, give_send, ring_send, ring_recv, sum_recv, back_send, back_recv,
    flat_send, flat_recv, plane_send, plane_recv, parts_send, parts_recv, flat_sum_send, flat_sum_recv,
    flat_back_send, flat_back_recv,
):
    section, me = lax.axis_index("section"), lax.axis_index("expert")
    following, leading = lax.rem(section + 1, sections), lax.rem(section + sections - 1, sections)
    group, z = me // RING, lax.rem(me, RING)
    tokens, width = act.shape
    rows = EXPERTS * capacity
    rest = width - FLAT
    half = RING // 2
    piece = tokens // PIECES
    last = RING - 1

    def along(k):
        return lax.rem(z + k, RING)

    def on_ring(k):
        return (section, group * RING + along(k))

    def in_plane(o, which):
        return (which, neighbour(group, o) * RING + z)

    smalls = [
        pltpu.make_async_copy(act_hbm.at[0], act, small_sem.at[0]),
        pltpu.make_async_copy(gain_hbm, gain, small_sem.at[1]),
        pltpu.make_async_copy(ids_hbm, ids, small_sem.at[2]),
    ]
    weights = [
        pltpu.make_async_copy(first_hbm.at[0], first, weight_sem.at[0]),
        pltpu.make_async_copy(second_hbm.at[0], second, weight_sem.at[1]),
    ]
    for copy in smalls:
        copy.start()
    barrier = pltpu.get_barrier_semaphore()
    greeted = [in_plane(o, section) for o in range(1, EXPERTS)] + [on_ring(1), on_ring(last)]
    greeted += [in_plane(o, leading) for o in range(EXPERTS)]
    for peer in greeted:
        pl.semaphore_signal(barrier, inc=1, device_id=peer, device_id_type=MESH)
    for copy in smalls:
        copy.wait()
    for copy in weights:
        copy.start()

    floats = act[...].astype(F32)
    scale = lax.rsqrt(jnp.mean(floats * floats, axis=-1, keepdims=True) + epsilon)
    values = (floats * scale * gain[...]).astype(BF16)
    normed[...] = values[:, FLAT:]
    flat[z, :, :, :FLAT] = values[:, :FLAT].reshape(PIECES, piece, FLAT)
    routed = ids[...]
    expert = lax.broadcasted_iota(jnp.int32, (EXPERTS, tokens), 0)
    onehot = jnp.where(expert == routed, 1.0, 0.0).astype(F32)
    earlier = lax.broadcasted_iota(jnp.int32, (tokens, tokens), 0) < lax.broadcasted_iota(
        jnp.int32, (tokens, tokens), 1
    )
    before = jnp.dot(
        onehot.astype(BF16), jnp.where(earlier, 1.0, 0.0).astype(BF16), preferred_element_type=F32
    )
    ranks = jnp.sum(before * onehot, axis=0, keepdims=True).astype(jnp.int32)
    placing = placement(routed, ranks, capacity, group, LANES)
    back = placing.T.astype(BF16)
    where_to[...] = back
    flat[z, :, :, FLAT:] = back.reshape(PIECES, piece, LANES)
    placing = placing[:rows].astype(BF16)

    pl.semaphore_wait(barrier, len(greeted))

    def forward_flat(block, c, k):
        pltpu.make_async_remote_copy(
            src_ref=flat.at[block, c], dst_ref=flat.at[block, c],
            send_sem=flat_send.at[0], recv_sem=flat_recv.at[block, c],
            device_id=on_ring(k), device_id_type=MESH,
        ).start()

    def forward(block, o, k, way):
        pltpu.make_async_remote_copy(
            src_ref=slots.at[block, o], dst_ref=slots.at[block, o],
            send_sem=ring_send.at[way], recv_sem=ring_recv.at[block, o],
            device_id=on_ring(k), device_id_type=MESH,
        ).start()

    for c in range(PIECES):
        forward_flat(z, c, 1)
        forward_flat(z, c, last)

    for c in range(rest // STEP):
        cols = slice(c * STEP, (c + 1) * STEP)
        block = jnp.dot(placing, normed[:, cols], preferred_element_type=F32)
        packed[:, :, cols] = block.astype(BF16).reshape(EXPERTS, capacity, STEP)
    slots[z, 0] = packed[0]
    for o in range(1, EXPERTS):
        pltpu.make_async_remote_copy(
            src_ref=packed.at[o], dst_ref=slots.at[z, mirrored(o)],
            send_sem=give_send.at[0], recv_sem=ring_recv.at[z, mirrored(o)],
            device_id=in_plane(o, section), device_id_type=MESH,
        ).start()
    forward(z, 0, 1, 0)
    forward(z, 0, last, 1)

    def routes(block):
        return flat[block, :, :, FLAT:].reshape(tokens, LANES)

    def pack(block):
        to_slot = routes(block).astype(F32).T[:rows].astype(BF16)
        for c in range(FLAT // STEP):
            cols = slice(c * STEP, (c + 1) * STEP)
            source = flat[block, :, :, cols].reshape(tokens, STEP)
            value = jnp.dot(to_slot, source, preferred_element_type=F32)
            value = value.astype(BF16).reshape(EXPERTS, capacity, STEP)
            spread_out[block, :, :, cols] = value
            spread_in[block, 0, :, cols] = value[0]
        for o in range(1, EXPERTS):
            pltpu.make_async_remote_copy(
                src_ref=spread_out.at[block, o], dst_ref=spread_in.at[block, mirrored(o)],
                send_sem=plane_send.at[0], recv_sem=plane_recv.at[block],
                device_id=in_plane(o, section), device_id_type=MESH,
            ).start()

    pack(z)
    passes = [
        pltpu.make_async_remote_copy(
            src_ref=src, dst_ref=dst, send_sem=pass_send.at[k], recv_sem=pass_recv.at[k],
            device_id=(following, me), device_id_type=MESH,
        )
        for k, (src, dst) in enumerate(((act.at[:, pl.ds(FLAT, rest)], residual), (where_to, where_from)))
    ]
    for copy in passes:
        copy.start()

    def ring_flat(k):
        left, right = along(RING - k), along(k)

        def hop(c, inner):
            arrived(flat.at[left, c], flat_recv.at[left, c])
            if k < half - 1:
                forward_flat(left, c, 1)
            if k < half:
                arrived(flat.at[right, c], flat_recv.at[right, c])
            if k < half - 1:
                forward_flat(right, c, last)
            if k == half - 1:
                @pl.when(c % 2 == 0)
                def _():
                    forward_flat(left, c, 1)

                @pl.when(c % 2 == 1)
                def _():
                    forward_flat(right, c, last)

            return inner

        lax.fori_loop(0, PIECES, hop, 0)

        def fill(i, inner):
            pack(along(jnp.where(i == 0, RING - k, k)))
            return inner

        lax.fori_loop(0, 2 if k < half else 1, fill, 0)

    def spread(o, carry):
        arrived(slots.at[z, o], ring_recv.at[z, o])
        forward(z, o, 1, 0)
        forward(z, o, last, 1)
        return carry

    def ring_slots(k, low, high):
        left, right = along(RING - k), along(k)

        def hop(o, inner):
            arrived(slots.at[left, o], ring_recv.at[left, o])

            @pl.when((k < half - 1) | ((k == half - 1) & (o % 2 == 0)))
            def _():
                forward(left, o, 1, 0)

            @pl.when(k < half)
            def _():
                arrived(slots.at[right, o], ring_recv.at[right, o])

            @pl.when((k < half - 1) | ((k == half - 1) & (o % 2 == 1)))
            def _():
                forward(right, o, last, 1)

            return inner

        lax.fori_loop(low, high, hop, 0)

    ring_flat(1)
    lax.fori_loop(1, EXPERTS // 2, spread, 0)
    ring_flat(2)
    lax.fori_loop(EXPERTS // 2, EXPERTS, spread, 0)
    ring_flat(3)
    ring_slots(jnp.int32(1), 0, EXPERTS // 2)
    ring_flat(4)
    ring_slots(jnp.int32(1), EXPERTS // 2, EXPERTS)
    for copy in weights:
        copy.wait()

    def pass_on(way, j, o, add):
        distance = half - j
        block = along(distance if way == 0 else RING - distance)
        value = partial[block, o]
        if add:
            arrived(arriving.at[way, j - 1, o], sum_recv.at[way, j - 1, o])
            value = value + arriving[way, j - 1, o].astype(F32)
        sending[way, j, o] = value.astype(BF16)
        pltpu.make_async_remote_copy(
            src_ref=sending.at[way, j, o], dst_ref=arriving.at[way, j, o],
            send_sem=ring_send.at[way], recv_sem=sum_recv.at[way, j, o],
            device_id=on_ring(1 if way == 0 else last), device_id_type=MESH,
        ).start()

    def pass_flat(way, j, c, add):
        distance = half - j
        block = along(distance if way == 0 else RING - distance)
        value = whole[block, c]
        if add:
            arrived(flat_arriving.at[way, j - 1, c], flat_sum_recv.at[way, j - 1, c])
            value = value + flat_arriving[way, j - 1, c].astype(F32)
        place = (way * half + j) * PIECES + c
        flat_sending[place] = value.astype(BF16)
        pltpu.make_async_remote_copy(
            src_ref=flat_sending.at[place], dst_ref=flat_arriving.at[way, j, c],
            send_sem=flat_sum_send.at[0], recv_sem=flat_sum_recv.at[way, j, c],
            device_id=on_ring(1 if way == 0 else last), device_id_type=MESH,
        ).start()

    def give_back(block):
        for o in range(1, EXPERTS):
            pltpu.make_async_remote_copy(
                src_ref=parts_out.at[block, o], dst_ref=parts_in.at[block, mirrored(o)],
                send_sem=parts_send.at[0], recv_sem=parts_recv.at[block],
                device_id=in_plane(o, section), device_id_type=MESH,
            ).start()

    def gather(k, carry):
        left, right = along(RING - k), along(k)

        @pl.when(k > 1)
        def _():
            ring_slots(k, 0, EXPERTS)

        other = jnp.where(k < half, right, z)
        for block in (left, other):
            others = spread_in.at[block, pl.ds(1, EXPERTS - 1)]
            arrived(others, plane_recv.at[block])
        flats = jnp.concatenate(
            [spread_in[left].reshape(rows, FLAT), spread_in[other].reshape(rows, FLAT)], axis=0
        )
        value = jnp.dot(flats, first[:FLAT], preferred_element_type=F32)
        inputs = jnp.concatenate(
            [slots[left].reshape(rows, rest), slots[other].reshape(rows, rest)], axis=0
        )
        value = value + jnp.dot(inputs, first[FLAT:], preferred_element_type=F32)
        hidden[...] = jax.nn.gelu(value, approximate=True).astype(BF16)

        def flat_tile(t, inner):
            cols = pl.ds(pl.multiple_of(t * STEP, STEP), STEP)
            result = jnp.dot(hidden[...], second[:, cols], preferred_element_type=F32)
            result = result.astype(BF16).reshape(2, EXPERTS, capacity, STEP)
            parts_out[left, :, :, cols] = result[0]
            parts_out[other, :, :, cols] = result[1]
            parts_in[left, 0, :, cols] = result[0, 0]
            parts_in[other, 0, :, cols] = result[1, 0]
            return inner

        lax.fori_loop(0, FLAT // STEP, flat_tile, 0)

        @pl.when(k != half - 2)
        def _():
            give_back(left)

        @pl.when((k == half - 3) | (k == half - 1))
        def _():
            give_back(other)

        def tile(t, inner):
            cols = pl.ds(pl.multiple_of(t * STEP, STEP), STEP)
            from_second = pl.ds(pl.multiple_of(FLAT + t * STEP, STEP), STEP)
            result = jnp.dot(hidden[...], second[:, from_second], preferred_element_type=F32)
            result = result.reshape(2, EXPERTS, capacity, STEP)
            partial[left, :, :, cols] = result[0]
            partial[other, :, :, cols] = result[1]
            return inner

        lax.fori_loop(0, rest // STEP, tile, 0)

        @pl.when(k == half - 1)
        def _():
            def early(i, inner):
                pass_on(0, 1, EXPERTS - 1 - 2 * i, False)
                pass_on(1, 1, EXPERTS - 2 - 2 * i, False)
                return inner

            lax.fori_loop(0, EXPERTS // 2, early, 0)

        return carry

    lax.fori_loop(1, half + 1, gather, 0)
    give_back(along(RING - 2))
    give_back(along(2))
    give_back(z)

    def start(i, carry):
        pass_on(0, 0, EXPERTS - 2 - 2 * i, False)
        pass_on(1, 0, EXPERTS - 1 - 2 * i, False)
        return carry

    lax.fori_loop(0, EXPERTS // 2, start, 0)

    def second_hop(i, carry):
        pass_on(0, 1, EXPERTS - 2 - 2 * i, True)
        pass_on(1, 1, EXPERTS - 1 - 2 * i, True)
        return carry

    lax.fori_loop(0, EXPERTS // 2, second_hop, 0)
    for j in range(2, half):
        def later(i, carry):
            pass_on(0, j, EXPERTS - 1 - i, True)
            pass_on(1, j, EXPERTS - 1 - i, True)
            return carry

        lax.fori_loop(0, EXPERTS, later, 0)

    def unpack(block):
        others = parts_in.at[block, pl.ds(1, EXPERTS - 1)]
        arrived(others, parts_recv.at[block])
        picks = routes(block)[:, :rows]
        for c in range(FLAT // STEP):
            cols = slice(c * STEP, (c + 1) * STEP)
            source = parts_in[block, :, :, cols].reshape(rows, STEP)
            value = jnp.dot(picks, source, preferred_element_type=F32)
            whole[block, :, :, cols] = value.reshape(PIECES, piece, STEP)

    def both(k):
        def one(i, carry):
            unpack(along(jnp.where(i == 0, RING - k, k)))
            return carry

        lax.fori_loop(0, 2, one, 0)

    unpack(along(half))
    for c in range(0, PIECES, 2):
        pass_flat(0, 0, c, False)
        pass_flat(1, 0, c + 1, False)
    both(half - 1)
    for c in range(0, PIECES, 2):
        pass_flat(0, 1, c + 1, False)
        pass_flat(1, 1, c, False)
    for c in range(0, PIECES, 2):
        pass_flat(0, 1, c, True)
        pass_flat(1, 1, c + 1, True)

    for o in reversed(range(EXPERTS)):
        value = partial[z, o]
        for way in range(2):
            arrived(arriving.at[way, half - 1, o], sum_recv.at[way, half - 1, o])
            value = value + arriving[way, half - 1, o].astype(F32)
        summed[o] = value.astype(BF16)
        pltpu.make_async_remote_copy(
            src_ref=summed.at[o], dst_ref=returned.at[mirrored(o)],
            send_sem=back_send.at[0], recv_sem=back_recv.at[0],
            device_id=in_plane(o, following), device_id_type=MESH,
        ).start()

    for j in range(2, half):
        both(half - j)
        for c in range(PIECES):
            pass_flat(0, j, c, True)
            pass_flat(1, j, c, True)
    unpack(z)
    for copy in passes:
        copy.wait()
    for c in range(PIECES):
        value = whole[z, c] + act[c * piece:(c + 1) * piece, :FLAT].astype(F32)
        for way in range(2):
            arrived(flat_arriving.at[way, half - 1, c], flat_sum_recv.at[way, half - 1, c])
            value = value + flat_arriving[way, half - 1, c].astype(F32)
        flat_summed[c] = value.astype(BF16)
        pltpu.make_async_remote_copy(
            src_ref=flat_summed.at[c], dst_ref=flat_returned.at[c],
            send_sem=flat_back_send.at[0], recv_sem=flat_back_recv.at[c],
            device_id=(following, me), device_id_type=MESH,
        ).start()

    arrived(returned, back_recv.at[0])
    picks = where_from[:, :rows]
    for c in range(rest // STEP):
        cols = slice(c * STEP, (c + 1) * STEP)
        to = slice(FLAT + c * STEP, FLAT + (c + 1) * STEP)
        mixed = jnp.dot(picks, returned[:, :, cols].reshape(rows, STEP), preferred_element_type=F32)
        out[0, :, to] = (residual[:, cols].astype(F32) + mixed).astype(BF16)
    for c in range(PIECES):
        arrived(flat_returned.at[c], flat_back_recv.at[c])
        out[0, c * piece:(c + 1) * piece, :FLAT] = flat_returned[c]

    arrived(packed.at[pl.ds(1, EXPERTS - 1)], give_send.at[0])
    for way in range(2):
        arrived(slots.at[pl.ds(0, RING - 1)], ring_send.at[way])
    arrived(flat.at[pl.ds(0, RING - 1)], flat_send.at[0])
    arrived(spread_out.at[pl.ds(0, RING - 1)], plane_send.at[0])
    arrived(parts_out.at[pl.ds(0, RING - 1)], parts_send.at[0])
    arrived(flat_sending.at[pl.ds(0, 2 * half * PIECES - PIECES)], flat_sum_send.at[0])
    arrived(summed, back_send.at[0])
    arrived(flat_summed, flat_back_send.at[0])


def per_device(sections, n, activations, norm_gain, in_proj, out_proj, expert_ids):
    tokens, width = activations.shape[1:]
    ff = in_proj.shape[2]
    capacity = 2 * tokens // EXPERTS
    rows = EXPERTS * capacity
    rest, piece, half = width - FLAT, tokens // PIECES, RING // 2
    dma = pltpu.SemaphoreType.DMA
    vmem = pltpu.VMEM
    return pl.pallas_call(
        functools.partial(kernel, sections, n, capacity),
        out_shape=pltpu.VMEM(activations.shape, activations.dtype),
        in_specs=[pl.BlockSpec(memory_space=pl.ANY)] * 5,
        out_specs=pl.BlockSpec(memory_space=pltpu.VMEM),
        scratch_shapes=[
            vmem((tokens, width), BF16),
            vmem((1, width), F32),
            vmem((1, tokens), jnp.int32),
            vmem((width, ff), BF16),
            vmem((ff, width), BF16),
            vmem((tokens, rest), BF16),
            vmem((EXPERTS, capacity, rest), BF16),
            vmem((RING, EXPERTS, capacity, rest), BF16),
            vmem((RING, PIECES, piece, FLAT + LANES), BF16),
            vmem((RING, EXPERTS, capacity, FLAT), BF16),
            vmem((RING, EXPERTS, capacity, FLAT), BF16),
            vmem((2 * rows, ff), BF16),
            vmem((RING, EXPERTS, capacity, rest), F32),
            vmem((2, half, EXPERTS, capacity, rest), BF16),
            vmem((2, half, EXPERTS, capacity, rest), BF16),
            vmem((EXPERTS, capacity, rest), BF16),
            vmem((EXPERTS, capacity, rest), BF16),
            vmem((RING, EXPERTS, capacity, FLAT), BF16),
            vmem((RING, EXPERTS, capacity, FLAT), BF16),
            vmem((RING, PIECES, piece, FLAT), F32),
            vmem((2 * half * PIECES, piece, FLAT), BF16),
            vmem((2, half, PIECES, piece, FLAT), BF16),
            vmem((PIECES, piece, FLAT), BF16),
            vmem((PIECES, piece, FLAT), BF16),
            vmem((tokens, LANES), BF16),
            vmem((tokens, rest), BF16),
            vmem((tokens, LANES), BF16),
            dma((3,)),
            dma((2,)),
            dma((2,)),
            dma((2,)),
            dma((1,)),
            dma((2,)),
            dma((RING, EXPERTS)),
            dma((2, half, EXPERTS)),
            dma((1,)),
            dma((1,)),
            dma((1,)),
            dma((RING, PIECES)),
            dma((1,)),
            dma((RING,)),
            dma((1,)),
            dma((RING,)),
            dma((1,)),
            dma((2, half, PIECES)),
            dma((1,)),
            dma((PIECES,)),
        ],
        compiler_params=pltpu.CompilerParams(
            collective_id=0, has_side_effects=True, vmem_limit_bytes=62 * 1024 * 1024
        ),
    )(activations, norm_gain, expert_ids.reshape(1, tokens), in_proj, out_proj)


def solution(mesh):
    return jax.shard_map(
        functools.partial(per_device, mesh.shape["section"], mesh.shape["expert"]),
        mesh=mesh,
        in_specs=(
            P("section", "expert", None),
            P("section", None),
            P("section", None, "expert"),
            P("section", "expert", None),
            P("section", "expert", None),
        ),
        out_specs=P("section", "expert", None),
        check_vma=False,
    )
```

time: 99.8 us -> 86.8 us (0.87)
  Pallas kernels: 99 us -> 86 us
    pallas_call x1, Pallas kernels: 99 us -> 86 us  [per_device(): pl.pallas_call(functools.partial(kernel, sections, n, capacity), out_shap...]
where the time goes in v2:
time: 86.8 us; the launch traced here: 86.7 us
  Pallas kernels  86 us (99%)
    pallas_call x1, Pallas kernels, per_device(): pl.pallas_call(functools.partial(kernel, sections, n, capacity), out_shap...  86 us

profile of v2, /device:TPU:1, one launch (start us, length us, event | category | flops | bytes accessed | tf_op | source)
XLA Modules:
  0.0 86.7 jit_solution(265219750746462658)
XLA Ops:
  0.0 86.0 %shard_map.55 = bf16[1,32,4096]{2,1,0:T(8,128)(2,1)S(1)} custom-call(bf16[1,32,4096]{2,1,0:T(8,128)(2,1)} %act_hbm.1, f32[1,4096]{1,0:T(1,128)} %gain_hbm.1, s32[1,32]{1,0:T(1,128)} %bitcast.1, bf16[1,4096,640]{2,1,0:T(8,128)(2,1)} %first_hbm.1, bf16[1,640,4096]{2,1,0:T(8,128)(2,1)} %second_hbm.1), custom_call_target="tpu_custom_call" | custom-call | tf_op jit(solution)/shard_map/pallas_call | solution.py:468
  86.0 0.7 copy.7

commit v3 on v2

--- a/solution.py
+++ b/solution.py
@@ -46,7 +46,7 @@
 
 def kernel(
     sections, n, capacity, act_hbm, gain_hbm, ids_hbm, first_hbm, second_hbm, out,
-    act, gain, ids, first, second, normed, packed, slots, flat, spread_out, spread_in, hidden,
+    act, gain, ids, first, second, normed, packed, slots, flat, spread_out, spread_in, total, hidden,
     partial, sending, arriving, summed, returned,
     parts_out, parts_in, whole, flat_sending, flat_arriving, flat_summed, flat_returned,
     where_to, residual, where_from,
@@ -179,7 +179,28 @@
     for copy in passes:
         copy.start()
 
-    def ring_flat(k):
+    def spread(o):
+        arrived(slots.at[z, o], ring_recv.at[z, o])
+        forward(z, o, 1, 0)
+        forward(z, o, last, 1)
+
+    def ring_slot(k, o):
+        left, right = along(RING - k), along(k)
+        arrived(slots.at[left, o], ring_recv.at[left, o])
+
+        @pl.when((k < half - 1) | ((k == half - 1) & (o % 2 == 0)))
+        def _():
+            forward(left, o, 1, 0)
+
+        @pl.when(k < half)
+        def _():
+            arrived(slots.at[right, o], ring_recv.at[right, o])
+
+        @pl.when((k < half - 1) | ((k == half - 1) & (o % 2 == 1)))
+        def _():
+            forward(right, o, last, 1)
+
+    def ring_flat(k, beside):
         left, right = along(RING - k), along(k)
 
         def hop(c, inner):
@@ -199,6 +220,7 @@
                 def _():
                     forward_flat(right, c, last)
 
+            beside(c)
             return inner
 
         lax.fori_loop(0, PIECES, hop, 0)
@@ -209,42 +231,15 @@
 
         lax.fori_loop(0, 2 if k < half else 1, fill, 0)
 
-    def spread(o, carry):
-        arrived(slots.at[z, o], ring_recv.at[z, o])
-        forward(z, o, 1, 0)
-        forward(z, o, last, 1)
-        return carry
-
-    def ring_slots(k, low, high):
-        left, right = along(RING - k), along(k)
-
-        def hop(o, inner):
-            arrived(slots.at[left, o], ring_recv.at[left, o])
-
-            @pl.when((k < half - 1) | ((k == half - 1) & (o % 2 == 0)))
-            def _():
-                forward(left, o, 1, 0)
-
-            @pl.when(k < half)
-            def _():
-                arrived(slots.at[right, o], ring_recv.at[right, o])
-
-            @pl.when((k < half - 1) | ((k == half - 1) & (o % 2 == 1)))
-            def _():
-                forward(right, o, last, 1)
-
-            return inner
-
-        lax.fori_loop(low, high, hop, 0)
-
-    ring_flat(1)
-    lax.fori_loop(1, EXPERTS // 2, spread, 0)
-    ring_flat(2)
-    lax.fori_loop(EXPERTS // 2, EXPERTS, spread, 0)
-    ring_flat(3)
-    ring_slots(jnp.int32(1), 0, EXPERTS // 2)
-    ring_flat(4)
-    ring_slots(jnp.int32(1), EXPERTS // 2, EXPERTS)
+    def near(c):
+        @pl.when(c > 0)
+        def _():
+            spread(c)
+
+    ring_flat(1, near)
+    ring_flat(2, lambda c: spread(PIECES + c))
+    ring_flat(3, lambda c: ring_slot(jnp.int32(1), c))
+    ring_flat(4, lambda c: ring_slot(jnp.int32(1), PIECES + c))
     for copy in weights:
         copy.wait()
 
@@ -285,28 +280,24 @@
                 device_id=in_plane(o, section), device_id_type=MESH,
             ).start()
 
-    def gather(k, carry):
-        left, right = along(RING - k), along(k)
-
-        @pl.when(k > 1)
-        def _():
-            ring_slots(k, 0, EXPERTS)
-
-        other = jnp.where(k < half, right, z)
+    def first_flat(left, other):
         for block in (left, other):
             others = spread_in.at[block, pl.ds(1, EXPERTS - 1)]
             arrived(others, plane_recv.at[block])
-        flats = jnp.concatenate(
+        inputs = jnp.concatenate(
             [spread_in[left].reshape(rows, FLAT), spread_in[other].reshape(rows, FLAT)], axis=0
         )
-        value = jnp.dot(flats, first[:FLAT], preferred_element_type=F32)
+        total[...] = jnp.dot(inputs, first[:FLAT], preferred_element_type=F32)
+
+    def first_slots(left, other):
         inputs = jnp.concatenate(
             [slots[left].reshape(rows, rest), slots[other].reshape(rows, rest)], axis=0
         )
-        value = value + jnp.dot(inputs, first[FLAT:], preferred_element_type=F32)
+        value = total[...] + jnp.dot(inputs, first[FLAT:], preferred_element_type=F32)
         hidden[...] = jax.nn.gelu(value, approximate=True).astype(BF16)
 
-        def flat_tile(t, inner):
+    def second_flat(left, other, low, high):
+        def tile(t, inner):
             cols = pl.ds(pl.multiple_of(t * STEP, STEP), STEP)
             result = jnp.dot(hidden[...], second[:, cols], preferred_element_type=F32)
             result = result.astype(BF16).reshape(2, EXPERTS, capacity, STEP)
@@ -316,16 +307,9 @@
             parts_in[other, 0, :, cols] = result[1, 0]
             return inner
 
-        lax.fori_loop(0, FLAT // STEP, flat_tile, 0)
-
-        @pl.when(k != half - 2)
-        def _():
-            give_back(left)
-
-        @pl.when((k == half - 3) | (k == half - 1))
-        def _():
-            give_back(other)
-
+        lax.fori_loop(low, high, tile, 0)
+
+    def second_slots(left, other, low, high):
         def tile(t, inner):
             cols = pl.ds(pl.multiple_of(t * STEP, STEP), STEP)
             from_second = pl.ds(pl.multiple_of(FLAT + t * STEP, STEP), STEP)
@@ -335,30 +319,90 @@
             partial[other, :, :, cols] = result[1]
             return inner
 
-        lax.fori_loop(0, rest // STEP, tile, 0)
+        lax.fori_loop(low, high, tile, 0)
+
+    flat_tiles, slot_tiles = FLAT // STEP, rest // STEP
+
+    def stage(k, carry):
+        left, right = along(RING - (k - 1)), along(k - 1)
+
+        def hop(o, inner):
+            ring_slot(k, o)
+
+            @pl.when(o == 0)
+            def _():
+                first_flat(left, right)
+
+            @pl.when(o == 1)
+            def _():
+                first_slots(left, right)
+
+            @pl.when((o > 1) & (o < 6))
+            def _():
+                i = o - 2
+                second_flat(left, right, i * flat_tiles // 4, (i + 1) * flat_tiles // 4)
+                second_slots(left, right, i * slot_tiles // 4, (i + 1) * slot_tiles // 4)
+
+            return inner
+
+        lax.fori_loop(0, EXPERTS, hop, 0)
+
+        @pl.when(k == 2)
+        def _():
+            give_back(left)
+            give_back(right)
+
+        return carry
+
+    lax.fori_loop(2, half, stage, 0)
+
+    def finish(k, carry):
+        left, right = along(RING - k), along(k)
+        other = jnp.where(k < half, right, z)
+
+        @pl.when(k == half)
+        def _():
+            def land(o, inner):
+                arrived(slots.at[left, o], ring_recv.at[left, o])
+                return inner
+
+            lax.fori_loop(0, EXPERTS, land, 0)
+
+        first_flat(left, other)
+        first_slots(left, other)
+        second_slots(left, other, 0, slot_tiles)
+
+        def early(i, inner):
+            pass_on(0, 1, EXPERTS - 1 - 2 * i, False)
+            pass_on(1, 1, EXPERTS - 2 - 2 * i, False)
+            return inner
+
+        def start(i, inner):
+            pass_on(0, 0, EXPERTS - 2 - 2 * i, False)
+            pass_on(1, 0, EXPERTS - 1 - 2 * i, False)
+            return inner
 
         @pl.when(k == half - 1)
         def _():
-            def early(i, inner):
-                pass_on(0, 1, EXPERTS - 1 - 2 * i, False)
-                pass_on(1, 1, EXPERTS - 2 - 2 * i, False)
-                return inner
-
             lax.fori_loop(0, EXPERTS // 2, early, 0)
 
+        @pl.when(k == half)
+        def _():
+            lax.fori_loop(0, EXPERTS // 2, start, 0)
+
+        second_flat(left, other, 0, flat_tiles)
+        give_back(left)
+
+        @pl.when(k == half - 1)
+        def _():
+            give_back(other)
+
         return carry
 
-    lax.fori_loop(1, half + 1, gather, 0)
+    lax.fori_loop(half - 1, half + 1, finish, 0)
     give_back(along(RING - 2))
     give_back(along(2))
     give_back(z)
-
-    def start(i, carry):
-        pass_on(0, 0, EXPERTS - 2 - 2 * i, False)
-        pass_on(1, 0, EXPERTS - 1 - 2 * i, False)
-        return carry
-
-    lax.fori_loop(0, EXPERTS // 2, start, 0)
 
     def second_hop(i, carry):
         pass_on(0, 1, EXPERTS - 2 - 2 * i, True)
@@ -366,13 +410,22 @@
         return carry
 
     lax.fori_loop(0, EXPERTS // 2, second_hop, 0)
-    for j in range(2, half):
-        def later(i, carry):
+
+    def later(j):
+        def one(i, carry):
             pass_on(0, j, EXPERTS - 1 - i, True)
             pass_on(1, j, EXPERTS - 1 - i, True)
             return carry
 
-        lax.fori_loop(0, EXPERTS, later, 0)
+        lax.fori_loop(0, EXPERTS, one, 0)
+
+    def later_flat(j):
+        def one(c, carry):
+            pass_flat(0, j, c, True)
+            pass_flat(1, j, c, True)
+            return carry
+
+        lax.fori_loop(0, PIECES, one, 0)
 
     def unpack(block):
         others = parts_in.at[block, pl.ds(1, EXPERTS - 1)]
@@ -391,6 +444,7 @@
 
         lax.fori_loop(0, 2, one, 0)
 
+    later(2)
     unpack(along(half))
     for c in range(0, PIECES, 2):
         pass_flat(0, 0, c, False)
@@ -399,9 +453,12 @@
     for c in range(0, PIECES, 2):
         pass_flat(0, 1, c + 1, False)
         pass_flat(1, 1, c, False)
+    later(3)
     for c in range(0, PIECES, 2):
         pass_flat(0, 1, c, True)
         pass_flat(1, 1, c + 1, True)
+    both(2)
+    later_flat(2)
 
     for o in reversed(range(EXPERTS)):
         value = partial[z, o]
@@ -415,11 +472,8 @@
             device_id=in_plane(o, following), device_id_type=MESH,
         ).start()
 
-    for j in range(2, half):
-        both(half - j)
-        for c in range(PIECES):
-            pass_flat(0, j, c, True)
-            pass_flat(1, j, c, True)
+    both(1)
+    later_flat(3)
     unpack(z)
     for copy in passes:
         copy.wait()
@@ -482,6 +536,7 @@
             vmem((RING, PIECES, piece, FLAT + LANES), BF16),
             vmem((RING, EXPERTS, capacity, FLAT), BF16),
             vmem((RING, EXPERTS, capacity, FLAT), BF16),
+            vmem((2 * rows, ff), F32),
             vmem((2 * rows, ff), BF16),
             vmem((RING, EXPERTS, capacity, rest), F32),
             vmem((2, half, EXPERTS, capacity, rest), BF16),

time: 86.8 us -> 82.4 us (0.949)
  Pallas kernels: 86 us -> 81.6 us
    pallas_call x1, Pallas kernels: 86 us -> 81.6 us  [per_device(): pl.pallas_call(functools.partial(kernel, sections, n, capacity), out_shap...]
where the time goes in v3:
time: 82.4 us
  Pallas kernels  81.6 us (99%)
    pallas_call x1, Pallas kernels, per_device(): pl.pallas_call(functools.partial(kernel, sections, n, capacity), out_shap...  81.6 us

profile of v3, /device:TPU:1, one launch (start us, length us, event | category | flops | bytes accessed | tf_op | source)
XLA Modules:
  0.0 82.4 jit_solution(1926137171983315701)
XLA Ops:
  0.0 81.6 %shard_map.55 = bf16[1,32,4096]{2,1,0:T(8,128)(2,1)S(1)} custom-call(bf16[1,32,4096]{2,1,0:T(8,128)(2,1)} %act_hbm.1, f32[1,4096]{1,0:T(1,128)} %gain_hbm.1, s32[1,32]{1,0:T(1,128)} %bitcast.1, bf16[1,4096,640]{2,1,0:T(8,128)(2,1)} %first_hbm.1, bf16[1,640,4096]{2,1,0:T(8,128)(2,1)} %second_hbm.1), custom_call_target="tpu_custom_call" | custom-call | tf_op jit(solution)/shard_map/pallas_call | solution.py:522
  81.6 0.7 copy.7

commit v4 on v3

--- a/solution.py
+++ b/solution.py
@@ -10,10 +10,12 @@
 EXPERTS = 8
 RING = 8
 NX = 4
-FLAT = 2048
+FLAT = 2176
+BACK = 2048
 PIECES = 4
 LANES = 128
-STEP = 512
+FIRST_PACK, SLOT_PACK = 2176, 640
+BACK_STEP, SLOT_STEP = 2048, 1024
 NEAR = ((0, 0), (0, 1), (0, 3), (1, 0), (0, 2), (1, 1), (1, 3), (1, 2))
 MESH = pl.DeviceIdType.MESH
 F32, BF16 = jnp.float32, jnp.bfloat16
@@ -50,8 +52,8 @@
     partial, sending, arriving, summed, returned,
     parts_out, parts_in, whole, flat_sending, flat_arriving, flat_summed, flat_returned,
     where_to, residual, where_from,
-    small_sem, weight_sem, pass_send, pass_recv, give_send, ring_send, ring_recv, sum_recv, back_send, back_recv,
-    flat_send, flat_recv, plane_send, plane_recv, parts_send, parts_recv, flat_sum_send, flat_sum_recv,
+    small_sem, weight_sem, pass_send, pass_recv, give_send, ring_send, ring_recv, sum_send, back_send, back_recv,
+    flat_send, flat_recv, plane_send, plane_recv, parts_send, parts_recv, flat_sum_send,
     flat_back_send, flat_back_recv,
 ):
     section, me = lax.axis_index("section"), lax.axis_index("expert")
@@ -59,7 +61,7 @@
     group, z = me // RING, lax.rem(me, RING)
     tokens, width = act.shape
     rows = EXPERTS * capacity
-    rest = width - FLAT
+    rest, back_rest = width - FLAT, width - BACK
     half = RING // 2
     piece = tokens // PIECES
     last = RING - 1
@@ -124,10 +126,10 @@
             device_id=on_ring(k), device_id_type=MESH,
         ).start()
 
-    def forward(block, o, k, way):
+    def forward(block, o, k):
         pltpu.make_async_remote_copy(
             src_ref=slots.at[block, o], dst_ref=slots.at[block, o],
-            send_sem=ring_send.at[way], recv_sem=ring_recv.at[block, o],
+            send_sem=ring_send.at[0], recv_sem=ring_recv.at[block, o],
             device_id=on_ring(k), device_id_type=MESH,
         ).start()
 
@@ -135,10 +137,10 @@
         forward_flat(z, c, 1)
         forward_flat(z, c, last)
 
-    for c in range(rest // STEP):
-        cols = slice(c * STEP, (c + 1) * STEP)
+    for c in range(rest // SLOT_PACK):
+        cols = slice(c * SLOT_PACK, (c + 1) * SLOT_PACK)
         block = jnp.dot(placing, normed[:, cols], preferred_element_type=F32)
-        packed[:, :, cols] = block.astype(BF16).reshape(EXPERTS, capacity, STEP)
+        packed[:, :, cols] = block.astype(BF16).reshape(EXPERTS, capacity, SLOT_PACK)
     slots[z, 0] = packed[0]
     for o in range(1, EXPERTS):
         pltpu.make_async_remote_copy(
@@ -146,19 +148,19 @@
             send_sem=give_send.at[0], recv_sem=ring_recv.at[z, mirrored(o)],
             device_id=in_plane(o, section), device_id_type=MESH,
         ).start()
-    forward(z, 0, 1, 0)
-    forward(z, 0, last, 1)
+    forward(z, 0, 1)
+    forward(z, 0, last)
 
     def routes(block):
         return flat[block, :, :, FLAT:].reshape(tokens, LANES)
 
     def pack(block):
         to_slot = routes(block).astype(F32).T[:rows].astype(BF16)
-        for c in range(FLAT // STEP):
-            cols = slice(c * STEP, (c + 1) * STEP)
-            source = flat[block, :, :, cols].reshape(tokens, STEP)
+        for c in range(FLAT // FIRST_PACK):
+            cols = slice(c * FIRST_PACK, (c + 1) * FIRST_PACK)
+            source = flat[block, :, :, cols].reshape(tokens, FIRST_PACK)
             value = jnp.dot(to_slot, source, preferred_element_type=F32)
-            value = value.astype(BF16).reshape(EXPERTS, capacity, STEP)
+            value = value.astype(BF16).reshape(EXPERTS, capacity, FIRST_PACK)
             spread_out[block, :, :, cols] = value
             spread_in[block, 0, :, cols] = value[0]
         for o in range(1, EXPERTS):
@@ -174,15 +176,15 @@
             src_ref=src, dst_ref=dst, send_sem=pass_send.at[k], recv_sem=pass_recv.at[k],
             device_id=(following, me), device_id_type=MESH,
         )
-        for k, (src, dst) in enumerate(((act.at[:, pl.ds(FLAT, rest)], residual), (where_to, where_from)))
+        for k, (src, dst) in enumerate(((act.at[:, pl.ds(BACK, back_rest)], residual), (where_to, where_from)))
     ]
     for copy in passes:
         copy.start()
 
     def spread(o):
         arrived(slots.at[z, o], ring_recv.at[z, o])
-        forward(z, o, 1, 0)
-        forward(z, o, last, 1)
+        forward(z, o, 1)
+        forward(z, o, last)
 
     def ring_slot(k, o):
         left, right = along(RING - k), along(k)
@@ -190,7 +192,7 @@
 
         @pl.when((k < half - 1) | ((k == half - 1) & (o % 2 == 0)))
         def _():
-            forward(left, o, 1, 0)
+            forward(left, o, 1)
 
         @pl.when(k < half)
         def _():
@@ -198,7 +200,7 @@
 
         @pl.when((k < half - 1) | ((k == half - 1) & (o % 2 == 1)))
         def _():
-            forward(right, o, last, 1)
+            forward(right, o, last)
 
     def ring_flat(k, beside):
         left, right = along(RING - k), along(k)
@@ -243,17 +245,24 @@
     for copy in weights:
         copy.wait()
 
+    def sum_sem(way, j, o, shift):
+        return ring_recv.at[along((j + shift) if way == 0 else (2 * RING - j - shift)), o]
+
+    def flat_sum_sem(way, j, c):
+        return flat_recv.at[way * half + j, c]
+
     def pass_on(way, j, o, add):
         distance = half - j
         block = along(distance if way == 0 else RING - distance)
         value = partial[block, o]
         if add:
-            arrived(arriving.at[way, j - 1, o], sum_recv.at[way, j - 1, o])
+            arrived(arriving.at[way, j - 1, o], sum_sem(way, j - 1, o, 0))
             value = value + arriving[way, j - 1, o].astype(F32)
-        sending[way, j, o] = value.astype(BF16)
-        pltpu.make_async_remote_copy(
-            src_ref=sending.at[way, j, o], dst_ref=arriving.at[way, j, o],
-            send_sem=ring_send.at[way], recv_sem=sum_recv.at[way, j, o],
+        place = (way * half + j) * EXPERTS + o
+        sending[place] = value.astype(BF16)
+        pltpu.make_async_remote_copy(
+            src_ref=sending.at[place], dst_ref=arriving.at[way, j, o],
+            send_sem=sum_send.at[0], recv_sem=sum_sem(way, j, o, 1),
             device_id=on_ring(1 if way == 0 else last), device_id_type=MESH,
         ).start()
 
@@ -262,13 +271,13 @@
         block = along(distance if way == 0 else RING - distance)
         value = whole[block, c]
         if add:
-            arrived(flat_arriving.at[way, j - 1, c], flat_sum_recv.at[way, j - 1, c])
+            arrived(flat_arriving.at[way, j - 1, c], flat_sum_sem(way, j - 1, c))
             value = value + flat_arriving[way, j - 1, c].astype(F32)
         place = (way * half + j) * PIECES + c
         flat_sending[place] = value.astype(BF16)
         pltpu.make_async_remote_copy(
             src_ref=flat_sending.at[place], dst_ref=flat_arriving.at[way, j, c],
-            send_sem=flat_sum_send.at[0], recv_sem=flat_sum_recv.at[way, j, c],
+            send_sem=flat_sum_send.at[0], recv_sem=flat_sum_sem(way, j, c),
             device_id=on_ring(1 if way == 0 else last), device_id_type=MESH,
         ).start()
 
@@ -298,9 +307,9 @@
 
     def second_flat(left, other, low, high):
         def tile(t, inner):
-            cols = pl.ds(pl.multiple_of(t * STEP, STEP), STEP)
+            cols = pl.ds(pl.multiple_of(t * BACK_STEP, BACK_STEP), BACK_STEP)
             result = jnp.dot(hidden[...], second[:, cols], preferred_element_type=F32)
-            result = result.astype(BF16).reshape(2, EXPERTS, capacity, STEP)
+            result = result.astype(BF16).reshape(2, EXPERTS, capacity, BACK_STEP)
             parts_out[left, :, :, cols] = result[0]
             parts_out[other, :, :, cols] = result[1]
             parts_in[left, 0, :, cols] = result[0, 0]
@@ -311,17 +320,17 @@
 
     def second_slots(left, other, low, high):
         def tile(t, inner):
-            cols = pl.ds(pl.multiple_of(t * STEP, STEP), STEP)
-            from_second = pl.ds(pl.multiple_of(FLAT + t * STEP, STEP), STEP)
+            cols = pl.ds(pl.multiple_of(t * SLOT_STEP, SLOT_STEP), SLOT_STEP)
+            from_second = pl.ds(pl.multiple_of(BACK + t * SLOT_STEP, SLOT_STEP), SLOT_STEP)
             result = jnp.dot(hidden[...], second[:, from_second], preferred_element_type=F32)
-            result = result.reshape(2, EXPERTS, capacity, STEP)
+            result = result.reshape(2, EXPERTS, capacity, SLOT_STEP)
             partial[left, :, :, cols] = result[0]
             partial[other, :, :, cols] = result[1]
             return inner
 
         lax.fori_loop(low, high, tile, 0)
 
-    flat_tiles, slot_tiles = FLAT // STEP, rest // STEP
+    flat_tiles, slot_tiles = BACK // BACK_STEP, back_rest // SLOT_STEP
 
     def stage(k, carry):
         left, right = along(RING - (k - 1)), along(k - 1)
@@ -347,11 +356,6 @@
 
         lax.fori_loop(0, EXPERTS, hop, 0)
 
-        @pl.when(k == 2)
-        def _():
-            give_back(left)
-            give_back(right)
-
         return carry
 
     lax.fori_loop(2, half, stage, 0)
@@ -402,6 +406,8 @@
     lax.fori_loop(half - 1, half + 1, finish, 0)
     give_back(along(RING - 2))
     give_back(along(2))
+    give_back(along(last))
+    give_back(along(1))
     give_back(z)
 
     def second_hop(i, carry):
@@ -411,13 +417,13 @@
 
     lax.fori_loop(0, EXPERTS // 2, second_hop, 0)
 
-    def later(j):
+    def later(j, low, high):
         def one(i, carry):
             pass_on(0, j, EXPERTS - 1 - i, True)
             pass_on(1, j, EXPERTS - 1 - i, True)
             return carry
 
-        lax.fori_loop(0, EXPERTS, one, 0)
+        lax.fori_loop(low, high, one, 0)
 
     def later_flat(j):
         def one(c, carry):
@@ -431,11 +437,11 @@
         others = parts_in.at[block, pl.ds(1, EXPERTS - 1)]
         arrived(others, parts_recv.at[block])
         picks = routes(block)[:, :rows]
-        for c in range(FLAT // STEP):
-            cols = slice(c * STEP, (c + 1) * STEP)
-            source = parts_in[block, :, :, cols].reshape(rows, STEP)
+        for c in range(BACK // BACK_STEP):
+            cols = slice(c * BACK_STEP, (c + 1) * BACK_STEP)
+            source = parts_in[block, :, :, cols].reshape(rows, BACK_STEP)
             value = jnp.dot(picks, source, preferred_element_type=F32)
-            whole[block, :, :, cols] = value.reshape(PIECES, piece, STEP)
+            whole[block, :, :, cols] = value.reshape(PIECES, piece, BACK_STEP)
 
     def both(k):
         def one(i, carry):
@@ -444,26 +450,27 @@
 
         lax.fori_loop(0, 2, one, 0)
 
-    later(2)
+    both(half - 1)
+    for c in range(0, PIECES, 2):
+        pass_flat(0, 1, c + 1, False)
+        pass_flat(1, 1, c, False)
+    later(2, 0, EXPERTS)
     unpack(along(half))
     for c in range(0, PIECES, 2):
         pass_flat(0, 0, c, False)
         pass_flat(1, 0, c + 1, False)
-    both(half - 1)
-    for c in range(0, PIECES, 2):
-        pass_flat(0, 1, c + 1, False)
-        pass_flat(1, 1, c, False)
-    later(3)
+    later(3, 0, EXPERTS // 2)
     for c in range(0, PIECES, 2):
         pass_flat(0, 1, c, True)
         pass_flat(1, 1, c + 1, True)
+    later(3, EXPERTS // 2, EXPERTS)
     both(2)
     later_flat(2)
 
     for o in reversed(range(EXPERTS)):
         value = partial[z, o]
         for way in range(2):
-            arrived(arriving.at[way, half - 1, o], sum_recv.at[way, half - 1, o])
+            arrived(arriving.at[way, half - 1, o], sum_sem(way, half - 1, o, 0))
             value = value + arriving[way, half - 1, o].astype(F32)
         summed[o] = value.astype(BF16)
         pltpu.make_async_remote_copy(
@@ -478,9 +485,9 @@
     for copy in passes:
         copy.wait()
     for c in range(PIECES):
-        value = whole[z, c] + act[c * piece:(c + 1) * piece, :FLAT].astype(F32)
+        value = whole[z, c] + act[c * piece:(c + 1) * piece, :BACK].astype(F32)
         for way in range(2):
-            arrived(flat_arriving.at[way, half - 1, c], flat_sum_recv.at[way, half - 1, c])
+            arrived(flat_arriving.at[way, half - 1, c], flat_sum_sem(way, half - 1, c))
             value = value + flat_arriving[way, half - 1, c].astype(F32)
         flat_summed[c] = value.astype(BF16)
         pltpu.make_async_remote_copy(
@@ -491,18 +498,18 @@
 
     arrived(returned, back_recv.at[0])
     picks = where_from[:, :rows]
-    for c in range(rest // STEP):
-        cols = slice(c * STEP, (c + 1) * STEP)
-        to = slice(FLAT + c * STEP, FLAT + (c + 1) * STEP)
-        mixed = jnp.dot(picks, returned[:, :, cols].reshape(rows, STEP), preferred_element_type=F32)
+    for c in range(back_rest // SLOT_STEP):
+        cols = slice(c * SLOT_STEP, (c + 1) * SLOT_STEP)
+        to = slice(BACK + c * SLOT_STEP, BACK + (c + 1) * SLOT_STEP)
+        mixed = jnp.dot(picks, returned[:, :, cols].reshape(rows, SLOT_STEP), preferred_element_type=F32)
         out[0, :, to] = (residual[:, cols].astype(F32) + mixed).astype(BF16)
     for c in range(PIECES):
         arrived(flat_returned.at[c], flat_back_recv.at[c])
-        out[0, c * piece:(c + 1) * piece, :FLAT] = flat_returned[c]
+        out[0, c * piece:(c + 1) * piece, :BACK] = flat_returned[c]
 
     arrived(packed.at[pl.ds(1, EXPERTS - 1)], give_send.at[0])
-    for way in range(2):
-        arrived(slots.at[pl.ds(0, RING - 1)], ring_send.at[way])
+    arrived(slots.at[pl.ds(0, RING - 1)], ring_send.at[0])
+    arrived(sending.at[pl.ds(0, 2 * half * EXPERTS - EXPERTS)], sum_send.at[0])
     arrived(flat.at[pl.ds(0, RING - 1)], flat_send.at[0])
     arrived(spread_out.at[pl.ds(0, RING - 1)], plane_send.at[0])
     arrived(parts_out.at[pl.ds(0, RING - 1)], parts_send.at[0])
@@ -516,7 +523,7 @@
     ff = in_proj.shape[2]
     capacity = 2 * tokens // EXPERTS
     rows = EXPERTS * capacity
-    rest, piece, half = width - FLAT, tokens // PIECES, RING // 2
+    rest, back_rest, piece, half = width - FLAT, width - BACK, tokens // PIECES, RING // 2
     dma = pltpu.SemaphoreType.DMA
     vmem = pltpu.VMEM
     return pl.pallas_call(
@@ -538,29 +545,29 @@
             vmem((RING, EXPERTS, capacity, FLAT), BF16),
             vmem((2 * rows, ff), F32),
             vmem((2 * rows, ff), BF16),
-            vmem((RING, EXPERTS, capacity, rest), F32),
-            vmem((2, half, EXPERTS, capacity, rest), BF16),
-            vmem((2, half, EXPERTS, capacity, rest), BF16),
-            vmem((EXPERTS, capacity, rest), BF16),
-            vmem((EXPERTS, capacity, rest), BF16),
-            vmem((RING, EXPERTS, capacity, FLAT), BF16),
-            vmem((RING, EXPERTS, capacity, FLAT), BF16),
-            vmem((RING, PIECES, piece, FLAT), F32),
-            vmem((2 * half * PIECES, piece, FLAT), BF16),
-            vmem((2, half, PIECES, piece, FLAT), BF16),
-            vmem((PIECES, piece, FLAT), BF16),
-            vmem((PIECES, piece, FLAT), BF16),
+            vmem((RING, EXPERTS, capacity, back_rest), F32),
+            vmem((2 * half * EXPERTS, capacity, back_rest), BF16),
+            vmem((2, half, EXPERTS, capacity, back_rest), BF16),
+            vmem((EXPERTS, capacity, back_rest), BF16),
+            vmem((EXPERTS, capacity, back_rest), BF16),
+            vmem((RING, EXPERTS, capacity, BACK), BF16),
+            vmem((RING, EXPERTS, capacity, BACK), BF16),
+            vmem((RING, PIECES, piece, BACK), F32),
+            vmem((2 * half * PIECES, piece, BACK), BF16),
+            vmem((2, half, PIECES, piece, BACK), BF16),
+            vmem((PIECES, piece, BACK), BF16),
+            vmem((PIECES, piece, BACK), BF16),
             vmem((tokens, LANES), BF16),
-            vmem((tokens, rest), BF16),
+            vmem((tokens, back_rest), BF16),
             vmem((tokens, LANES), BF16),
             dma((3,)),
             dma((2,)),
             dma((2,)),
             dma((2,)),
             dma((1,)),
-            dma((2,)),
+            dma((1,)),
             dma((RING, EXPERTS)),
-            dma((2, half, EXPERTS)),
+            dma((1,)),
             dma((1,)),
             dma((1,)),
             dma((1,)),
@@ -570,7 +577,6 @@
             dma((1,)),
             dma((RING,)),
             dma((1,)),
-            dma((2, half, PIECES)),
             dma((1,)),
             dma((PIECES,)),
         ],

time: 82.4 us -> 79.8 us (0.968)
  Pallas kernels: 81.6 us -> 79 us
    pallas_call x1, Pallas kernels: 81.6 us -> 79 us  [per_device(): pl.pallas_call(functools.partial(kernel, sections, n, capacity), out_shap...]
where the time goes in v4:
time: 79.8 us
  Pallas kernels  79 us (99%)
    pallas_call x1, Pallas kernels, per_device(): pl.pallas_call(functools.partial(kernel, sections, n, capacity), out_shap...  79 us

profile of v4, /device:TPU:1, one launch (start us, length us, event | category | flops | bytes accessed | tf_op | source)
XLA Modules:
  0.0 79.8 jit_solution(6642956113940137797)
XLA Ops:
  0.0 79.0 %shard_map.55 = bf16[1,32,4096]{2,1,0:T(8,128)(2,1)S(1)} custom-call(bf16[1,32,4096]{2,1,0:T(8,128)(2,1)} %act_hbm.1, f32[1,4096]{1,0:T(1,128)} %gain_hbm.1, s32[1,32]{1,0:T(1,128)} %bitcast.1, bf16[1,4096,640]{2,1,0:T(8,128)(2,1)} %first_hbm.1, bf16[1,640,4096]{2,1,0:T(8,128)(2,1)} %second_hbm.1), custom_call_target="tpu_custom_call" | custom-call | tf_op jit(solution)/shard_map/pallas_call | solution.py:529
  79.1 0.7 copy.7

commit v5 on v4

--- a/solution.py
+++ b/solution.py
@@ -54,7 +54,7 @@
     where_to, residual, where_from,
     small_sem, weight_sem, pass_send, pass_recv, give_send, ring_send, ring_recv, sum_send, back_send, back_recv,
     flat_send, flat_recv, plane_send, plane_recv, parts_send, parts_recv, flat_sum_send,
-    flat_back_send, flat_back_recv,
+    flat_back_send, flat_back_recv, beyond,
 ):
     section, me = lax.axis_index("section"), lax.axis_index("expert")
     following, leading = lax.rem(section + 1, sections), lax.rem(section + sections - 1, sections)
@@ -87,8 +87,7 @@
     for copy in smalls:
         copy.start()
     barrier = pltpu.get_barrier_semaphore()
-    greeted = [in_plane(o, section) for o in range(1, EXPERTS)] + [on_ring(1), on_ring(last)]
-    greeted += [in_plane(o, leading) for o in range(EXPERTS)]
+    greeted = [in_plane(o, section) for o in range(1, 4)] + [on_ring(1), on_ring(last), in_plane(0, leading)]
     for peer in greeted:
         pl.semaphore_signal(barrier, inc=1, device_id=peer, device_id_type=MESH)
     for copy in smalls:
@@ -133,6 +132,8 @@
             device_id=on_ring(k), device_id_type=MESH,
         ).start()
 
+    for o in (1, 2):
+        pl.semaphore_signal(beyond.at[0], inc=1, device_id=in_plane(o, section), device_id_type=MESH)
     for c in range(PIECES):
         forward_flat(z, c, 1)
         forward_flat(z, c, last)
@@ -142,19 +143,27 @@
         block = jnp.dot(placing, normed[:, cols], preferred_element_type=F32)
         packed[:, :, cols] = block.astype(BF16).reshape(EXPERTS, capacity, SLOT_PACK)
     slots[z, 0] = packed[0]
-    for o in range(1, EXPERTS):
+
+    def give(o):
         pltpu.make_async_remote_copy(
             src_ref=packed.at[o], dst_ref=slots.at[z, mirrored(o)],
             send_sem=give_send.at[0], recv_sem=ring_recv.at[z, mirrored(o)],
             device_id=in_plane(o, section), device_id_type=MESH,
         ).start()
+
+    for o in (1, 2, 3):
+        give(o)
     forward(z, 0, 1)
     forward(z, 0, last)
+    pl.semaphore_wait(beyond.at[0], 2)
+    pl.semaphore_signal(beyond.at[1], inc=1, device_id=in_plane(3, section), device_id_type=MESH)
+    for o in (4, 5, 6):
+        give(o)
 
     def routes(block):
         return flat[block, :, :, FLAT:].reshape(tokens, LANES)
 
-    def pack(block):
+    def pack(block, first=False):
         to_slot = routes(block).astype(F32).T[:rows].astype(BF16)
         for c in range(FLAT // FIRST_PACK):
             cols = slice(c * FIRST_PACK, (c + 1) * FIRST_PACK)
@@ -163,6 +172,9 @@
             value = value.astype(BF16).reshape(EXPERTS, capacity, FIRST_PACK)
             spread_out[block, :, :, cols] = value
             spread_in[block, 0, :, cols] = value[0]
+        if first:
+            pl.semaphore_wait(beyond.at[1], 1)
+            give(7)
         for o in range(1, EXPERTS):
             pltpu.make_async_remote_copy(
                 src_ref=spread_out.at[block, o], dst_ref=spread_in.at[block, mirrored(o)],
@@ -170,7 +182,7 @@
                 device_id=in_plane(o, section), device_id_type=MESH,
             ).start()
 
-    pack(z)
+    pack(z, first=True)
     passes = [
         pltpu.make_async_remote_copy(
             src_ref=src, dst_ref=dst, send_sem=pass_send.at[k], recv_sem=pass_recv.at[k],
@@ -579,6 +591,7 @@
             dma((1,)),
             dma((1,)),
             dma((PIECES,)),
+            pltpu.SemaphoreType.REGULAR((2,)),
         ],
         compiler_params=pltpu.CompilerParams(
             collective_id=0, has_side_effects=True, vmem_limit_bytes=62 * 1024 * 1024

time: 79.8 us -> 79.2 us (level)
  no operation moved by 1% of the time
where the time goes in v5:
time: 79.2 us; the launch traced here: 79.1 us
  Pallas kernels  78.4 us (99%)
    pallas_call x1, Pallas kernels, per_device(): pl.pallas_call(functools.partial(kernel, sections, n, capacity), out_shap...  78.4 us

profile of v5, /device:TPU:1, one launch (start us, length us, event | category | flops | bytes accessed | tf_op | source)
XLA Modules:
  0.0 79.1 jit_solution(936352649195898750)
XLA Ops:
  0.0 78.4 %shard_map.55 = bf16[1,32,4096]{2,1,0:T(8,128)(2,1)S(1)} custom-call(bf16[1,32,4096]{2,1,0:T(8,128)(2,1)} %act_hbm.1, f32[1,4096]{1,0:T(1,128)} %gain_hbm.1, s32[1,32]{1,0:T(1,128)} %bitcast.1, bf16[1,4096,640]{2,1,0:T(8,128)(2,1)} %first_hbm.1, bf16[1,640,4096]{2,1,0:T(8,128)(2,1)} %second_hbm.1), custom_call_target="tpu_custom_call" | custom-call | tf_op jit(solution)/shard_map/pallas_call | solution.py:541
  78.4 0.7 copy.7

commit v6 on v5

--- a/solution.py
+++ b/solution.py
@@ -462,15 +462,15 @@
 
         lax.fori_loop(0, 2, one, 0)
 
-    both(half - 1)
-    for c in range(0, PIECES, 2):
-        pass_flat(0, 1, c + 1, False)
-        pass_flat(1, 1, c, False)
     later(2, 0, EXPERTS)
     unpack(along(half))
     for c in range(0, PIECES, 2):
         pass_flat(0, 0, c, False)
         pass_flat(1, 0, c + 1, False)
+    both(half - 1)
+    for c in range(0, PIECES, 2):
+        pass_flat(0, 1, c + 1, False)
+        pass_flat(1, 1, c, False)
     later(3, 0, EXPERTS // 2)
     for c in range(0, PIECES, 2):
         pass_flat(0, 1, c, True)

time: 79.2 us -> 78 us (0.985)
  Pallas kernels: 78.4 us -> 77.2 us
    pallas_call x1, Pallas kernels: 78.4 us -> 77.2 us  [per_device(): pl.pallas_call(functools.partial(kernel, sections, n, capacity), out_shap...]
where the time goes in v6:
time: 78 us; the launch traced here: 77.9 us
  Pallas kernels  77.2 us (99%)
    pallas_call x1, Pallas kernels, per_device(): pl.pallas_call(functools.partial(kernel, sections, n, capacity), out_shap...  77.2 us

profile of v6, /device:TPU:1, one launch (start us, length us, event | category | flops | bytes accessed | tf_op | source)
XLA Modules:
  0.0 77.9 jit_solution(1053659230238728854)
XLA Ops:
  0.0 77.2 %shard_map.55 = bf16[1,32,4096]{2,1,0:T(8,128)(2,1)S(1)} custom-call(bf16[1,32,4096]{2,1,0:T(8,128)(2,1)} %act_hbm.1, f32[1,4096]{1,0:T(1,128)} %gain_hbm.1, s32[1,32]{1,0:T(1,128)} %bitcast.1, bf16[1,4096,640]{2,1,0:T(8,128)(2,1)} %first_hbm.1, bf16[1,640,4096]{2,1,0:T(8,128)(2,1)} %second_hbm.1), custom_call_target="tpu_custom_call" | custom-call | tf_op jit(solution)/shard_map/pallas_call | solution.py:541
  77.2 0.7 copy.7
